TPU v7x, 32 devices: a whole 2x2x4 slice. The times are simulated.
32 devices in a mesh: rep: 4 (over y, x), shard: 8 (over z, core).
Axes of the slice: x: 2, y: 2, z: 4, core: 2. Of those that a mesh axis runs over, the one named last changes fastest.
Arguments:
- hot_ids: int32 [65536], P(('rep', 'shard')), may hold values from 0 to 8191
- hot_grads: bfloat16 [65536, 128], P(('rep', 'shard')), may hold values from -6 to 6
- hot_rows: float32 [8192, 128], replicated, may hold values from -6 to 6
- hot_accum: float32 [8192], replicated, may hold values from 0.5 to 4
- cold_counts: int32 [32, 32], P(('rep', 'shard')), may hold values from 1 to 16, as said below
- cold_slots: int32 [32, 32, 16], P(('rep', 'shard')), may hold values from 0 to 8191
- cold_grads: bfloat16 [32, 32, 16, 128], P(('rep', 'shard')), may hold values from -6 to 6
- cold_rows: float32 [262144, 128], P(('rep', 'shard')), may hold values from -6 to 6
- cold_accum: float32 [262144], P(('rep', 'shard')), may hold values from 0.5 to 4
Outputs:
- new_hot_rows: float32 [8192, 128], replicated
- new_hot_accum: float32 [8192], replicated
- new_cold_rows: float32 [262144, 128], P(('rep', 'shard'))
- new_cold_accum: float32 [262144], P(('rep', 'shard'))
Inputs may be any that keep to these rules, and one draw needn't show every extreme that they name: `cold_counts`: every entry is at least 1 and at most 16; in every draw some owner receives 16 live slots from every sender.
All inputs are finite; a program needn't handle non-finite values.
Results may differ from a plain program's by a relative error of at most 0.0003.
Values may be sent and summed in bfloat16 or wider, within the bound.
A program may use at most 128 MiB of HBM per device.

v0:
```python
import jax
import jax.numpy as jnp
from jax import lax
from jax.sharding import PartitionSpec as P

learn_rate = 0.5


def adagrad(table_rows, accum_rows, gradient):
    accum_new = accum_rows + jnp.mean(gradient * gradient, axis=1)
    return (table_rows - learn_rate * gradient / jnp.sqrt(accum_new)[:, None], accum_new)


def local(
    hot_ids,
    hot_grads,
    hot_rows,
    hot_accum,
    cold_counts,
    cold_slots,
    cold_grads,
    cold_rows,
    cold_accum,
):
    hot_count = hot_rows.shape[0]
    dense = jax.ops.segment_sum(hot_grads.astype(jnp.float32), hot_ids, num_segments=hot_count)
    share = hot_count // lax.axis_size("shard")
    part_sum = lax.psum_scatter(dense, "shard", scatter_dimension=0, tiled=True)
    part_sum = lax.psum(part_sum, "rep")
    start = lax.axis_index("shard") * share
    rows_share = lax.dynamic_slice_in_dim(hot_rows, start, share, 0)
    accum_share = lax.dynamic_slice_in_dim(hot_accum, start, share, 0)
    rows_new, accum_new = adagrad(rows_share, accum_share, part_sum)
    new_hot_rows, new_hot_accum = (
        lax.all_gather(rows_new, "shard", axis=0, tiled=True),
        lax.all_gather(accum_new, "shard", axis=0, tiled=True),
    )
    received, slots_in, counts_in = (
        lax.all_to_all(cold_grads, ("rep", "shard"), split_axis=1, concat_axis=0, tiled=True),
        lax.all_to_all(cold_slots, ("rep", "shard"), split_axis=1, concat_axis=0, tiled=True),
        lax.all_to_all(cold_counts, ("rep", "shard"), split_axis=1, concat_axis=0, tiled=True),
    )
    width = received.shape[-1]
    capacity = received.shape[2]
    slot_index = lax.broadcasted_iota(jnp.int32, (1, 1, capacity), 2)
    live_mask = slot_index < counts_in[:, :, None]
    masked_terms = jnp.where(live_mask[..., None], received.astype(jnp.float32), 0.0)
    local_rows = cold_rows.shape[0]
    cold_sum = jax.ops.segment_sum(
        masked_terms.reshape(-1, width), slots_in.reshape(-1), num_segments=local_rows
    )
    new_cold_rows, new_cold_accum = adagrad(cold_rows, cold_accum, cold_sum)
    return (new_hot_rows, new_hot_accum, new_cold_rows, new_cold_accum)


def solution(mesh):
    placed = (
        P(("rep", "shard")),
        P(("rep", "shard"), None),
        P(),
        P(),
        P(("rep", "shard"), None),
        P(("rep", "shard"), None, None),
        P(("rep", "shard"), None, None, None),
        P(("rep", "shard"), None),
        P(("rep", "shard")),
    )
    return jax.shard_map(
        local,
        mesh=mesh,
        in_specs=placed,
        out_specs=(P(), P(), P(("rep", "shard"), None), P(("rep", "shard"))),
        check_vma=False,
    )
```

profile of v0, /device:TPU:0, one launch (start us, length us, event | category | flops | bytes accessed | tf_op | source)
XLA Modules:
  0.0 199.6 jit_solution(5830766798041887270)
XLA Ops:
  7.2 0.0 reduce-scatter.2.cloned.1.call-start
  7.2 14.1 %scatter_custom_fusion = f32[8192,128]{1,0:T(8,128)} fusion(s32[2048]{0:T(1024)} %param.9, f32[]{:T(128)} %constant.3.clone.1, bf16[2048,128]{1,0:T(8,128)(2,1)} %param.10), kind=kCustom, calls=%fused_computation.6 | custom fusion | flops 524288 | bytes 4719104 | tf_op jit(solution)/shard_map/scatter-add | solution.py:26
  21.3 0.0 copy-start.3
  21.3 0.0 copy-start.2
  21.3 0.0 reduce-scatter.2.cloned.1.call-update
  21.3 0.0 all-reduce.2.cloned.1.call-start
  21.4 52.8 %reduce-scatter.2.cloned.1.call-done = f32[1024,128]{1,0:T(8,128)} async-done(((f32[8192,128]{1,0:T(8,128)}), f32[1024,128]{1,0:T(8,128)}) %reduce-scatter.2.cloned.1.call-update) | async-done | bytes 524304 | tf_op jit(solution)/shard_map/reduce_scatter | solution.py:28
  74.1 0.0 all-reduce.2.cloned.1.call-update
  74.2 0.0 all-gather.2.cloned.1.call-start
  74.2 46.8 %all-reduce.2.cloned.1.call-done = f32[1024,128]{1,0:T(8,128)} async-done(((f32[1024,128]{1,0:T(8,128)}), f32[1024,128]{1,0:T(8,128)}) %all-reduce.2.cloned.1.call-update) | async-done | bytes 524304 | tf_op jit(solution)/shard_map/psum | solution.py:29
  121.0 1.2 multiply_reduce_fusion.1
  122.2 0.7 fusion.8
  122.9 2.2 %divide_subtract_fusion.1 = f32[1024,128]{1,0:T(8,128)} fusion(f32[1024,128]{1,0:T(8,128)} %all-reduce.2.cloned.1.call-done, f32[8192,128]{1,0:T(8,128)} %param.11, s32[]{:T(128)S(6)} %select_n.11, f32[1024]{0:T(1024)S(1)} %get-tuple-element.6), kind=kLoop, calls=%fused_computation.9 | loop fusion | flops 393216 | bytes 1576964 | tf_op jit(solution)/shard_map/sub | solution.py:11
  125.1 0.0 all-gather.2.cloned.1.call-update
  125.2 0.0 copy-done.3
  125.2 0.7 copy.18
  125.9 4.6 %all-to-all-start.1 = ((s32[1,32,1]{2,0,1:T(1,128)}), s32[1,32,1]{2,0,1:T(1,128)S(1)}, u32[]{:S(2)}, u32[]{:S(2)}) async-start(s32[1,32,1]{2,0,1:T(1,128)} %copy.18), calls=%async_computation.2 | async-start | bytes 32768 | tf_op jit(solution)/shard_map/all_to_all | solution.py:41
  130.5 0.0 copy-done.2
  130.5 0.1 copy.17
  130.6 7.0 %all-to-all-done.1 = s32[1,32,1]{2,0,1:T(1,128)S(1)} async-done(((s32[1,32,1]{2,0,1:T(1,128)}), s32[1,32,1]{2,0,1:T(1,128)S(1)}, u32[]{:S(2)}, u32[]{:S(2)}) %all-to-all-start.1) | async-done | bytes 160 | tf_op jit(solution)/shard_map/all_to_all | solution.py:41
  137.6 9.1 %all_to_all.31 = s32[1,32,16]{2,0,1:T(1,128)S(1)} all-to-all(s32[1,32,16]{2,0,1:T(1,128)S(1)} %copy.17), channel_id=1, replica_groups=mesh['rep'=4,'shard'=8] {'rep','shard'}, dimensions={1} | all-to-all | bytes 4096 | tf_op jit(solution)/shard_map/all_to_all | solution.py:40
  146.7 2.6 %all-to-all-start.2 = ((bf16[1,32,16,128]{3,2,0,1:T(8,128)(2,1)}), bf16[1,32,16,128]{3,2,0,1:T(8,128)(2,1)S(1)}, u32[]{:S(2)}, u32[]{:S(2)}) async-start(bf16[1,32,16,128]{3,2,0,1:T(8,128)(2,1)} %bitcast.1), calls=%async_computation.3 | async-start | bytes 262144 | tf_op jit(solution)/shard_map/all_to_all | solution.py:39
  149.3 0.7 reduce.1
  150.0 0.1 iota_compare_fusion
  150.0 0.1 lt.33
  150.1 0.5 broadcast.40
  150.6 0.7 reduce.4
  151.3 0.1 reshape.77
  151.4 9.5 %all-to-all-done.2 = bf16[1,32,16,128]{3,2,0,1:T(8,128)(2,1)S(1)} async-done(((bf16[1,32,16,128]{3,2,0,1:T(8,128)(2,1)}), bf16[1,32,16,128]{3,2,0,1:T(8,128)(2,1)S(1)}, u32[]{:S(2)}, u32[]{:S(2)}) %all-to-all-start.2) | async-done | bytes 131104 | tf_op jit(solution)/shard_map/all_to_all | solution.py:39
  160.9 0.0 copy-start.1
  160.9 4.6 %scatter_custom_fusion.1 = f32[8192,128]{1,0:T(8,128)} fusion(s32[512]{0:T(512)S(1)} %reshape.77, f32[]{:T(128)} %constant.3.clone.1, bf16[512,128]{1,0:T(8,128)(2,1)S(1)} %bitcast.7, pred[512]{0:T(512)(128)(4,1)S(1)} %lt.33), kind=kCustom, calls=%fused_computation.4 | custom fusion | flops 196608 | bytes 4326912 | tf_op jit(solution)/shard_map/scatter-add | solution.py:49
  165.5 0.0 copy-start
  165.5 3.5 %multiply_reduce_fusion = f32[8192]{0:T(1024)S(1)} fusion(f32[8192,128]{1,0:T(8,128)} %scatter_custom_fusion.1), kind=kLoop, calls=%fused_computation.3 | loop fusion | flops 2088960 | bytes 4227072 | tf_op jit(solution)/shard_map/reduce_sum | solution.py:10
  169.0 0.0 copy-done.1
  169.1 0.6 fusion.7
  169.7 0.0 copy-done
  169.7 4.2 %divide_subtract_fusion = f32[8192,128]{1,0:T(8,128)} fusion(f32[8192,128]{1,0:T(8,128)} %param.16, f32[8192,128]{1,0:T(8,128)S(1)} %copy-done, f32[8192]{0:T(1024)S(1)} %get-tuple-element.4), kind=kLoop, calls=%fused_computation.2 | loop fusion | flops 3145728 | bytes 12615680 | tf_op jit(solution)/shard_map/sub | solution.py:11
  173.9 14.1 %all_gather.7 = f32[8192]{0:T(1024)S(1)} all-gather(f32[1024]{0:T(1024)S(1)} %get-tuple-element.7), channel_id=1, replica_groups=mesh['rep'=4,'shard'=8] {'shard'}, dimensions={0}, use_global_device_ids=true | all-gather | bytes 36864 | tf_op jit(solution)/shard_map/all_gather | solution.py:36
  188.0 0.0 all-gather.2.cloned.1.call-done
  188.0 4.5 %copy.23 = f32[8192,128]{1,0:T(8,128)} copy(f32[8192,128]{1,0:T(8,128)} %all-gather.2.cloned.1.call-done) | data formatting | bytes 8388608
  192.4 0.6 copy.24
Async XLA Ops:
  7.2 67.0 %reduce-scatter.2.cloned.1.call-start = ((), (), s32[]{:S(2)}) async-start(), calls=%async_computation.4 | async-start | bytes 4718592 | tf_op jit(solution)/shard_map/reduce_scatter | solution.py:28
  21.3 103.9 %copy-start.3 = (s32[1,32]{1,0:T(1,128)S(1)}, s32[1,32]{1,0:T(1,128)}, u32[]{:S(2)}) copy-start(s32[1,32]{1,0:T(1,128)} %param.13) | copy-start | bytes 388
  21.3 109.2 %copy-start.2 = (s32[1,32,16]{1,2,0:T(8,128)S(1)}, s32[1,32,16]{1,2,0:T(8,128)}, u32[]{:S(2)}) copy-start(s32[1,32,16]{1,2,0:T(8,128)} %param.14) | copy-start | bytes 6148
  21.3 99.7 %all-reduce.2.cloned.1.call-start = ((), (), s32[]{:S(2)}) async-start(), calls=%async_computation.5 | async-start | bytes 1048576 | tf_op jit(solution)/shard_map/psum | solution.py:29
  74.2 113.8 %all-gather.2.cloned.1.call-start = ((), (), s32[]{:S(2)}) async-start(), calls=%async_computation.6 | async-start | bytes 4718592 | tf_op jit(solution)/shard_map/all_gather | solution.py:35
  125.9 11.7 %all-to-all-start.1 = ((s32[1,32,1]{2,0,1:T(1,128)}), s32[1,32,1]{2,0,1:T(1,128)S(1)}, u32[]{:S(2)}, u32[]{:S(2)}) async-start(s32[1,32,1]{2,0,1:T(1,128)} %copy.18), calls=%async_computation.2 | async-start | bytes 32768 | tf_op jit(solution)/shard_map/all_to_all | solution.py:41
  146.7 14.2 %all-to-all-start.2 = ((bf16[1,32,16,128]{3,2,0,1:T(8,128)(2,1)}), bf16[1,32,16,128]{3,2,0,1:T(8,128)(2,1)S(1)}, u32[]{:S(2)}, u32[]{:S(2)}) async-start(bf16[1,32,16,128]{3,2,0,1:T(8,128)(2,1)} %bitcast.1), calls=%async_computation.3 | async-start | bytes 262144 | tf_op jit(solution)/shard_map/all_to_all | solution.py:39
  160.9 8.1 %copy-start.1 = (f32[8192]{0:T(1024)S(1)}, f32[8192]{0:T(1024)}, u32[]{:S(2)}) copy-start(f32[8192]{0:T(1024)} %param.17) | copy-start | bytes 98308
  165.5 4.1 %copy-start = (f32[8192,128]{1,0:T(8,128)S(1)}, f32[8192,128]{1,0:T(8,128)}, u32[]{:S(2)}) copy-start(f32[8192,128]{1,0:T(8,128)} %scatter_custom_fusion.1) | copy-start | bytes 12582916
Sparse Core Ops, SparseCore 0:
  21.4 52.6 reduce-scatter.1
  77.1 43.8 all-reduce.1
  125.3 50.0 all-gather.1
where the time goes:
time: 200 us
  waiting for transfers between devices  116 us (58%)
  other arithmetic  32.6 us (16%)
  blocking collectives  23.2 us (12%)
  between operations  13.8 us (7%)
  starting transfers between devices  7.29 us (4%)
  local copies, waits for them, and re-layouts  6.56 us (3%)
    reduce_scatter x1, waiting for transfers between devices, local(): part_sum = lax.psum_scatter(dense, 'shard', scatter_dimension=0, tiled=True)  52.8 us
    psum x1, waiting for transfers between devices, local(): part_sum = lax.psum(part_sum, 'rep')  46.8 us
    scatter-add x1, other arithmetic, local(): jax.ops.segment_sum(hot_grads.astype(jnp.float32), hot_ids, num_segments=...  14.1 us
    all_gather x1, blocking collectives, local(): lax.all_gather(accum_new, 'shard', axis=0, tiled=True)  14.1 us
    all_to_all x1, waiting for transfers between devices, local(): lax.all_to_all(cold_grads, ('rep', 'shard'), split_axis=1, concat_axis=0,...  9.51 us
    all_to_all x1, blocking collectives, local(): lax.all_to_all(cold_slots, ('rep', 'shard'), split_axis=1, concat_axis=0,...  9.13 us
    all_to_all x1, waiting for transfers between devices, local(): lax.all_to_all(cold_counts, ('rep', 'shard'), split_axis=1, concat_axis=0...  7.01 us
    sub x2, other arithmetic, adagrad(): table_rows - learn_rate * gradient / jnp.sqrt(accum_new)[:, None]  6.43 us
  transfers between devices with their start and end apart: 5, of which 4 were waited for; matrix products, arithmetic and copies ran while one was open for 8% of the time, Pallas kernels for 0%

commit v1 on v0

--- a/solution.py
+++ b/solution.py
@@ -26,7 +26,9 @@
     dense = jax.ops.segment_sum(hot_grads.astype(jnp.float32), hot_ids, num_segments=hot_count)
     share = hot_count // lax.axis_size("shard")
     part_sum = lax.psum_scatter(dense, "shard", scatter_dimension=0, tiled=True)
-    part_sum = lax.psum(part_sum, "rep")
+    part_sum = part_sum
+    for hop in (1, 2):
+        part_sum = part_sum + lax.ppermute(part_sum, "rep", [(dev, dev ^ hop) for dev in range(4)])
     start = lax.axis_index("shard") * share
     rows_share = lax.dynamic_slice_in_dim(hot_rows, start, share, 0)
     accum_share = lax.dynamic_slice_in_dim(hot_accum, start, share, 0)

time: 200 us -> 180 us (0.900)
  waiting for transfers between devices: 116 us -> 89.3 us
  starting transfers between devices: 7.29 us -> 13.4 us
    psum x1 -> x0, waiting for transfers between devices: 46.8 us -> none  [local(): part_sum = lax.psum(part_sum, 'rep')]
    ppermute x0 -> x2, waiting for transfers between devices: none -> 20 us  [local(): lax.ppermute(part_sum, 'rep', [(dev, dev ^ hop) for dev in range(4)])]
    all_to_all x1, starting transfers between devices: 4.6 us -> 7.72 us  [local(): lax.all_to_all(cold_counts, ('rep', 'shard'), split_axis=1, concat_axis=0...]
    ppermute x0 -> x2, starting transfers between devices: none -> 2.99 us  [local(): lax.ppermute(part_sum, 'rep', [(dev, dev ^ hop) for dev in range(4)])]
  transfers between devices with their start and end apart: 5 -> 6, of which waited for: 4 -> 5; matrix products, arithmetic and copies ran while one was open for 8% -> 9% of each run, Pallas kernels for 0% -> 0%
where the time goes in v1:
time: 180 us; the launch traced here: 179 us
  waiting for transfers between devices  89.3 us (50%)
  other arithmetic  32.5 us (18%)
  blocking collectives  23.2 us (13%)
  between operations  14.1 us (8%)
  starting transfers between devices  13.4 us (7%)
  local copies, waits for them, and re-layouts  6.56 us (4%)
    reduce_scatter x1, waiting for transfers between devices, local(): part_sum = lax.psum_scatter(dense, 'shard', scatter_dimension=0, tiled=True)  52.8 us
    ppermute x2, waiting for transfers between devices, local(): lax.ppermute(part_sum, 'rep', [(dev, dev ^ hop) for dev in range(4)])  20 us
    scatter-add x1, other arithmetic, local(): jax.ops.segment_sum(hot_grads.astype(jnp.float32), hot_ids, num_segments=...  14.1 us
    all_gather x1, blocking collectives, local(): lax.all_gather(accum_new, 'shard', axis=0, tiled=True)  14.1 us
    all_to_all x1, waiting for transfers between devices, local(): lax.all_to_all(cold_grads, ('rep', 'shard'), split_axis=1, concat_axis=0,...  9.51 us
    all_to_all x1, blocking collectives, local(): lax.all_to_all(cold_slots, ('rep', 'shard'), split_axis=1, concat_axis=0,...  9.13 us
    all_to_all x1, starting transfers between devices, local(): lax.all_to_all(cold_counts, ('rep', 'shard'), split_axis=1, concat_axis=0...  7.72 us
    all_to_all x1, waiting for transfers between devices, local(): lax.all_to_all(cold_counts, ('rep', 'shard'), split_axis=1, concat_axis=0...  7.02 us
  transfers between devices with their start and end apart: 6, of which 5 were waited for; matrix products, arithmetic and copies ran while one was open for 9% of the time, Pallas kernels for 0%

profile of v1, /device:TPU:0, one launch (start us, length us, event | category | flops | bytes accessed | tf_op | source)
XLA Modules:
  0.0 179.1 jit_solution(8736421293171864418)
XLA Ops:
  7.2 0.0 reduce-scatter.2.cloned.1.call-start
  7.2 14.1 %scatter_custom_fusion = f32[8192,128]{1,0:T(8,128)} fusion(s32[2048]{0:T(1024)} %param.9, f32[]{:T(128)} %constant.3.clone.1, bf16[2048,128]{1,0:T(8,128)(2,1)} %param.10), kind=kCustom, calls=%fused_computation.6 | custom fusion | flops 524288 | bytes 4719104 | tf_op jit(solution)/shard_map/scatter-add | solution.py:26
  21.3 0.0 copy-start.3
  21.3 0.0 copy-start.2
  21.3 0.0 reduce-scatter.2.cloned.1.call-update
  21.3 0.0 all-gather.2.cloned.1.call-start
  21.4 52.8 %reduce-scatter.2.cloned.1.call-done = f32[1024,128]{1,0:T(8,128)} async-done(((f32[8192,128]{1,0:T(8,128)}), f32[1024,128]{1,0:T(8,128)}) %reduce-scatter.2.cloned.1.call-update) | async-done | bytes 524304 | tf_op jit(solution)/shard_map/reduce_scatter | solution.py:28
  74.1 1.5 collective-permute-start
  75.6 10.6 %collective-permute-done = f32[1024,128]{1,0:T(8,128)S(1)} collective-permute-done((f32[1024,128]{1,0:T(8,128)}, f32[1024,128]{1,0:T(8,128)S(1)}, u32[]{:S(2)}, u32[]{:S(2)}) %collective-permute-start) | collective-permute-done | bytes 524320 | tf_op jit(solution)/shard_map/ppermute | solution.py:31
  86.1 1.1 add.23
  87.3 1.5 collective-permute-start.1
  88.8 9.5 %collective-permute-done.1 = f32[1024,128]{1,0:T(8,128)S(1)} collective-permute-done((f32[1024,128]{1,0:T(8,128)S(1)}, f32[1024,128]{1,0:T(8,128)S(1)}, u32[]{:S(2)}, u32[]{:S(2)}) %collective-permute-start.1) | collective-permute-done | bytes 524320 | tf_op jit(solution)/shard_map/ppermute | solution.py:31
  98.3 0.2 multiply_reduce_fusion.1
  98.5 0.7 fusion.8
  99.2 2.0 %divide_subtract_fusion.1 = f32[1024,128]{1,0:T(8,128)} fusion(f32[8192,128]{1,0:T(8,128)} %param.11, s32[]{:T(128)S(6)} %select_n.11, f32[1024]{0:T(1024)S(1)} %get-tuple-element.6, f32[1024,128]{1,0:T(8,128)S(1)} %add.23, f32[1024,128]{1,0:T(8,128)S(1)} %collective-permute-done.1), kind=kLoop, calls=%fused_computation.9 | loop fusion | flops 524288 | bytes 2101252 | tf_op jit(solution)/shard_map/sub | solution.py:11
  101.2 0.0 all-gather.2.cloned.1.call-update
  101.3 0.0 copy-done.3
  101.3 0.7 copy.18
  102.0 7.7 %all-to-all-start.1 = ((s32[1,32,1]{2,0,1:T(1,128)}), s32[1,32,1]{2,0,1:T(1,128)S(1)}, u32[]{:S(2)}, u32[]{:S(2)}) async-start(s32[1,32,1]{2,0,1:T(1,128)} %copy.18), calls=%async_computation.2 | async-start | bytes 32768 | tf_op jit(solution)/shard_map/all_to_all | solution.py:43
  109.7 0.0 copy-done.2
  109.7 0.1 copy.17
  109.8 7.0 %all-to-all-done.1 = s32[1,32,1]{2,0,1:T(1,128)S(1)} async-done(((s32[1,32,1]{2,0,1:T(1,128)}), s32[1,32,1]{2,0,1:T(1,128)S(1)}, u32[]{:S(2)}, u32[]{:S(2)}) %all-to-all-start.1) | async-done | bytes 160 | tf_op jit(solution)/shard_map/all_to_all | solution.py:43
  116.8 9.1 %all_to_all.31 = s32[1,32,16]{2,0,1:T(1,128)S(1)} all-to-all(s32[1,32,16]{2,0,1:T(1,128)S(1)} %copy.17), channel_id=1, replica_groups=mesh['rep'=4,'shard'=8] {'rep','shard'}, dimensions={1} | all-to-all | bytes 4096 | tf_op jit(solution)/shard_map/all_to_all | solution.py:42
  125.9 2.6 %all-to-all-start.2 = ((bf16[1,32,16,128]{3,2,0,1:T(8,128)(2,1)}), bf16[1,32,16,128]{3,2,0,1:T(8,128)(2,1)S(1)}, u32[]{:S(2)}, u32[]{:S(2)}) async-start(bf16[1,32,16,128]{3,2,0,1:T(8,128)(2,1)} %bitcast.1), calls=%async_computation.3 | async-start | bytes 262144 | tf_op jit(solution)/shard_map/all_to_all | solution.py:41
  128.5 0.7 reduce.1
  129.2 0.1 iota_compare_fusion
  129.2 0.1 lt.33
  129.3 0.5 broadcast.40
  129.9 0.7 reduce.4
  130.6 0.1 reshape.77
  130.6 9.5 %all-to-all-done.2 = bf16[1,32,16,128]{3,2,0,1:T(8,128)(2,1)S(1)} async-done(((bf16[1,32,16,128]{3,2,0,1:T(8,128)(2,1)}), bf16[1,32,16,128]{3,2,0,1:T(8,128)(2,1)S(1)}, u32[]{:S(2)}, u32[]{:S(2)}) %all-to-all-start.2) | async-done | bytes 131104 | tf_op jit(solution)/shard_map/all_to_all | solution.py:41
  140.1 0.0 copy-start.1
  140.1 4.6 %scatter_custom_fusion.1 = f32[8192,128]{1,0:T(8,128)} fusion(s32[512]{0:T(512)S(1)} %reshape.77, f32[]{:T(128)} %constant.3.clone.1, bf16[512,128]{1,0:T(8,128)(2,1)S(1)} %bitcast.7, pred[512]{0:T(512)(128)(4,1)S(1)} %lt.33), kind=kCustom, calls=%fused_computation.4 | custom fusion | flops 196608 | bytes 4326912 | tf_op jit(solution)/shard_map/scatter-add | solution.py:51
  144.7 0.0 copy-start
  144.8 3.5 %multiply_reduce_fusion = f32[8192]{0:T(1024)S(1)} fusion(f32[8192,128]{1,0:T(8,128)} %scatter_custom_fusion.1), kind=kLoop, calls=%fused_computation.3 | loop fusion | flops 2088960 | bytes 4227072 | tf_op jit(solution)/shard_map/reduce_sum | solution.py:10
  148.2 0.0 copy-done.1
  148.3 0.6 fusion.7
  148.9 0.0 copy-done
  148.9 4.2 %divide_subtract_fusion = f32[8192,128]{1,0:T(8,128)} fusion(f32[8192,128]{1,0:T(8,128)} %param.16, f32[8192,128]{1,0:T(8,128)S(1)} %copy-done, f32[8192]{0:T(1024)S(1)} %get-tuple-element.4), kind=kLoop, calls=%fused_computation.2 | loop fusion | flops 3145728 | bytes 12615680 | tf_op jit(solution)/shard_map/sub | solution.py:11
  153.1 14.1 %all_gather.7 = f32[8192]{0:T(1024)S(1)} all-gather(f32[1024]{0:T(1024)S(1)} %get-tuple-element.7), channel_id=1, replica_groups=mesh['rep'=4,'shard'=8] {'shard'}, dimensions={0}, use_global_device_ids=true | all-gather | bytes 36864 | tf_op jit(solution)/shard_map/all_gather | solution.py:38
  167.2 0.0 all-gather.2.cloned.1.call-done
  167.2 4.5 %copy.22 = f32[8192,128]{1,0:T(8,128)} copy(f32[8192,128]{1,0:T(8,128)} %all-gather.2.cloned.1.call-done) | data formatting | bytes 8388608
  171.6 0.6 copy.23
Async XLA Ops:
  7.2 67.0 %reduce-scatter.2.cloned.1.call-start = ((), (), s32[]{:S(2)}) async-start(), calls=%async_computation.4 | async-start | bytes 4718592 | tf_op jit(solution)/shard_map/reduce_scatter | solution.py:28
  21.3 80.0 %copy-start.3 = (s32[1,32]{1,0:T(1,128)S(1)}, s32[1,32]{1,0:T(1,128)}, u32[]{:S(2)}) copy-start(s32[1,32]{1,0:T(1,128)} %param.13) | copy-start | bytes 388
  21.3 88.4 %copy-start.2 = (s32[1,32,16]{1,2,0:T(8,128)S(1)}, s32[1,32,16]{1,2,0:T(8,128)}, u32[]{:S(2)}) copy-start(s32[1,32,16]{1,2,0:T(8,128)} %param.14) | copy-start | bytes 6148
  21.3 145.8 %all-gather.2.cloned.1.call-start = ((), (), s32[]{:S(2)}) async-start(), calls=%async_computation.5 | async-start | bytes 4718592 | tf_op jit(solution)/shard_map/all_gather | solution.py:37
  74.1 12.0 %collective-permute-start = (f32[1024,128]{1,0:T(8,128)}, f32[1024,128]{1,0:T(8,128)S(1)}, u32[]{:S(2)}, u32[]{:S(2)}) collective-permute-start(f32[1024,128]{1,0:T(8,128)} %reduce-scatter.2.cloned.1.call-done), channel_id=1, source_target_pairs={{0,8},{8,0},{16,24},{24,16},{1,9},{9,1},{17,25},{25,17},{2,10},{10... | collective-permute-start | bytes 1572872 | tf_op jit(solution)/shard_map/ppermute | solution.py:31
  87.3 11.0 %collective-permute-start.1 = (f32[1024,128]{1,0:T(8,128)S(1)}, f32[1024,128]{1,0:T(8,128)S(1)}, u32[]{:S(2)}, u32[]{:S(2)}) collective-permute-start(f32[1024,128]{1,0:T(8,128)S(1)} %add.23), channel_id=1, source_target_pairs={{0,16},{8,24},{16,0},{24,8},{1,17},{9,25},{17,1},{25,9},{2,18},{10... | collective-permute-start | bytes 1572872 | tf_op jit(solution)/shard_map/ppermute | solution.py:31
  102.0 14.8 %all-to-all-start.1 = ((s32[1,32,1]{2,0,1:T(1,128)}), s32[1,32,1]{2,0,1:T(1,128)S(1)}, u32[]{:S(2)}, u32[]{:S(2)}) async-start(s32[1,32,1]{2,0,1:T(1,128)} %copy.18), calls=%async_computation.2 | async-start | bytes 32768 | tf_op jit(solution)/shard_map/all_to_all | solution.py:43
  125.9 14.2 %all-to-all-start.2 = ((bf16[1,32,16,128]{3,2,0,1:T(8,128)(2,1)}), bf16[1,32,16,128]{3,2,0,1:T(8,128)(2,1)S(1)}, u32[]{:S(2)}, u32[]{:S(2)}) async-start(bf16[1,32,16,128]{3,2,0,1:T(8,128)(2,1)} %bitcast.1), calls=%async_computation.3 | async-start | bytes 262144 | tf_op jit(solution)/shard_map/all_to_all | solution.py:41
  140.1 8.1 %copy-start.1 = (f32[8192]{0:T(1024)S(1)}, f32[8192]{0:T(1024)}, u32[]{:S(2)}) copy-start(f32[8192]{0:T(1024)} %param.17) | copy-start | bytes 98308
  144.7 4.1 %copy-start = (f32[8192,128]{1,0:T(8,128)S(1)}, f32[8192,128]{1,0:T(8,128)}, u32[]{:S(2)}) copy-start(f32[8192,128]{1,0:T(8,128)} %scatter_custom_fusion.1) | copy-start | bytes 12582916
Sparse Core Ops, SparseCore 0:
  21.4 52.6 reduce-scatter.1
  101.4 53.1 all-gather.1
